TPU v7x, 256 devices: a whole 4x4x8 slice. The times are simulated.
256 devices in a mesh: dp: 32 (over y, x, core), mp: 8 (over z).
Axes of the slice: x: 4, y: 4, z: 8, core: 2. Of those that a mesh axis runs over, the one named last changes fastest.
Arguments:
- clean: bfloat16 [128, 256, 1536], P('dp', None, 'mp'), may hold values from -6 to 6
- noise: bfloat16 [128, 256, 1536], P('dp', None, 'mp'), may hold values from -6 to 6
- teacher_first: bfloat16 [128, 256, 1536], P('dp', None, 'mp'), may hold values from -6 to 6
- teacher_second: bfloat16 [128, 256, 1536], P('dp', None, 'mp'), may hold values from -6 to 6
- step_index: int32 [128], P('dp'), may hold values from 8 to 32
- teacher_count: int32 [128], P('dp'), may hold values from 64 to 256
- up_master: float32 [1536, 6144], P('dp', 'mp'), may hold values from -6 to 6
- down_master: float32 [1536, 6144], P('dp', 'mp'), may hold values from -6 to 6
- up_moment: float32 [1536, 6144], P('dp', 'mp'), may hold values from -1.8 to 1.8
- down_moment: float32 [1536, 6144], P('dp', 'mp'), may hold values from -1.8 to 1.8
- up_second: float32 [1536, 6144], P('dp', 'mp'), may hold values from 0.002 to 0.032
- down_second: float32 [1536, 6144], P('dp', 'mp'), may hold values from 0.002 to 0.032
Outputs:
- new_up_master: float32 [1536, 6144], P('dp', 'mp')
- new_down_master: float32 [1536, 6144], P('dp', 'mp')
- new_up_moment: float32 [1536, 6144], P('dp', 'mp')
- new_down_moment: float32 [1536, 6144], P('dp', 'mp')
- new_up_second: float32 [1536, 6144], P('dp', 'mp')
- new_down_second: float32 [1536, 6144], P('dp', 'mp')
- loss_mean: float32 [], replicated
Inputs may be any that keep to these rules, and one draw needn't show every extreme that they name: `step_index`: student step k with 2k at most the sample's teacher_count.
All inputs are finite; a program needn't handle non-finite values.
Results may differ from a plain program's by a relative error of at most 0.002.
Values may be sent and summed in bfloat16 or wider, within the bound.
No kernel may reach another device: no remote copies, remote signals or barrier semaphores. Data moves between devices by JAX's collectives and lax.ppermute only.
A program may use at most 64 MiB of HBM per device.

v0:
```python
import functools
import math
import jax
import jax.numpy as jnp
from jax import lax
from jax.sharding import Mesh
from jax.sharding import PartitionSpec as P

DP = ("dp_0", "dp_1", "dp_2")
DP_MP = ("dp_0", "dp_1", "dp_2", "mp")
adam_count = 100.0
learn_rate = 0.05
decay_rate = 0.01


def sent_together(arrays, axis, dim, along):
    both = jnp.concatenate(arrays, axis=along)
    result, at, outs = (lax.all_gather(both, axis, axis=dim, tiled=True), 0, [])
    for a in arrays:
        outs.append(lax.slice_in_dim(result, at, at + a.shape[along], axis=along))
        at += a.shape[along]
    return tuple(outs)


def sent_together_2(arrays, axis, dim, along):
    ends, at = ([], 0)
    for a in arrays[:-1]:
        at += a.shape[along]
        ends.append(at)
    both = jnp.concatenate(arrays, axis=along)
    return tuple(
        jnp.split(lax.psum_scatter(both, axis, scatter_dimension=dim, tiled=True), ends, axis=along)
    )


def by_axis(shard, axes):
    return functools.reduce(lax.psum, axes, shard)


def gelu_pair(preact):
    tanh_arg = 0.7978845608028654 * (preact + 0.044715 * preact * preact * preact)
    tanh_val = jnp.tanh(tanh_arg)
    activation = 0.5 * preact * (1.0 + tanh_val)
    slopes = 0.5 * (1.0 + tanh_val) + 0.5 * preact * (
        1.0 - tanh_val * tanh_val
    ) * 0.7978845608028654 * (1.0 + 3.0 * 0.044715 * preact * preact)
    return (activation, slopes)


def distill_target(clean, noise, teacher_first, teacher_second, step_index, teacher_count):
    steps_float = teacher_count.astype(jnp.float32)[:, None, None]
    doubled = 2.0 * step_index.astype(jnp.float32)[:, None, None]
    quarter_turn = 0.5 * math.pi
    time_now = doubled / steps_float
    time_mid = (doubled - 1.0) / steps_float
    time_end = (doubled - 2.0) / steps_float
    alpha_now = jnp.cos(quarter_turn * time_now)
    sigma_now = jnp.sin(quarter_turn * time_now)
    alpha_mid = jnp.cos(quarter_turn * time_mid)
    sigma_mid = jnp.sin(quarter_turn * time_mid)
    alpha_end = jnp.cos(quarter_turn * time_end)
    sigma_end = jnp.sin(quarter_turn * time_end)
    first_f = teacher_first.astype(jnp.float32)
    second_f = teacher_second.astype(jnp.float32)
    latent_now = alpha_now * clean.astype(jnp.float32) + sigma_now * noise.astype(jnp.float32)
    noise_now = (latent_now - alpha_now * first_f) / sigma_now
    latent_mid = alpha_mid * first_f + sigma_mid * noise_now
    noise_mid = (latent_mid - alpha_mid * second_f) / sigma_mid
    latent_end = alpha_end * second_f + sigma_end * noise_mid
    sigma_ratio = sigma_end / sigma_now
    target = (latent_end - sigma_ratio * latent_now) / (alpha_end - sigma_ratio * alpha_now)
    weighting = jnp.maximum(alpha_now * alpha_now / (sigma_now * sigma_now), 1.0)[:, 0, 0]
    return (latent_now, target, weighting)


def adam_update(master, moment, second, gradient, factor):
    clipped = gradient * factor
    moment_new = 0.9 * moment + 0.1 * clipped
    second_new = 0.999 * second + 0.001 * clipped * clipped
    first_hat = moment_new / (1.0 - 0.9**adam_count)
    second_hat = second_new / (1.0 - 0.999**adam_count)
    master_new = master - learn_rate * (
        first_hat / (jnp.sqrt(second_hat) + 1e-08) + decay_rate * master
    )
    return (master_new, moment_new, second_new)


def per_device(
    clean,
    noise,
    teacher_first,
    teacher_second,
    step_index,
    teacher_count,
    up_master,
    down_master,
    up_moment,
    down_moment,
    up_second,
    down_second,
):
    samples_dev, token_count, width_local = clean.shape
    sample_total = samples_dev * lax.axis_size(DP)
    row_count = samples_dev * token_count
    latent, target, weighting = distill_target(
        clean, noise, teacher_first, teacher_second, step_index, teacher_count
    )
    noisy_rows = latent.reshape(row_count, width_local).astype(jnp.bfloat16)
    gathered = lax.all_gather(noisy_rows, "mp", axis=1, tiled=True)
    gathered_f = gathered.astype(jnp.float32)
    normed = (
        gathered_f * lax.rsqrt(jnp.mean(gathered_f * gathered_f, axis=1, keepdims=True) + 1e-06)
    ).astype(jnp.bfloat16)
    up_full, down_full = sent_together(
        (up_master.astype(jnp.bfloat16), down_master.astype(jnp.bfloat16)), DP, 0, 1
    )
    width_full = up_full.shape[0]
    hidden_local = up_full.shape[1]
    dscale = width_full ** (-0.5)
    fscale = (hidden_local * lax.axis_size("mp")) ** (-0.5)
    preact = jnp.dot(normed, up_full, preferred_element_type=jnp.float32) * dscale
    activation, slopes = gelu_pair(preact)
    hidden = activation.astype(jnp.bfloat16)
    partial_value = (
        lax.dot_general(
            hidden, down_full, (((1,), (1,)), ((), ())), preferred_element_type=jnp.float32
        )
        * fscale
    )
    branch = lax.psum_scatter(
        partial_value.astype(jnp.bfloat16), "mp", scatter_dimension=1, tiled=True
    ).astype(jnp.float32)
    errors = latent + branch.reshape(latent.shape) - target
    weight_cube = weighting[:, None, None]
    loss_part = jnp.sum(weight_cube * errors * errors)
    dpred = (
        (2.0 * weight_cube / sample_total * errors)
        .astype(jnp.bfloat16)
        .reshape(row_count, width_local)
    )
    piece = lax.all_gather(dpred, "mp", axis=1, tiled=True)
    summed = jnp.dot(piece, down_full, preferred_element_type=jnp.float32)
    grad_piece = (
        lax.dot_general(piece, hidden, (((0,), (0,)), ((), ())), preferred_element_type=jnp.float32)
        * fscale
    )
    dpre = (summed * fscale * slopes).astype(jnp.bfloat16)
    grad_up = (
        lax.dot_general(normed, dpre, (((0,), (0,)), ((), ())), preferred_element_type=jnp.float32)
        * dscale
    )
    owned_up, owned_down = sent_together_2((grad_up, grad_piece), DP, 0, 1)
    squares = jnp.sum(owned_up * owned_up) + jnp.sum(owned_down * owned_down)
    loss_total, square_total = (by_axis(loss_part, DP_MP), by_axis(squares, DP_MP))
    clip_limit = math.sqrt(2.0 * width_full * hidden_local * lax.axis_size("mp"))
    factor = clip_limit / jnp.maximum(jnp.sqrt(square_total), clip_limit)
    new_up, up_m, up_v = adam_update(up_master, up_moment, up_second, owned_up, factor)
    new_down, down_m, down_v = adam_update(
        down_master, down_moment, down_second, owned_down, factor
    )
    loss_mean = loss_total / (sample_total * token_count * width_full)
    return (new_up, new_down, up_m, down_m, up_v, down_v, loss_mean)


def solution(mesh):
    split = Mesh(mesh.devices.reshape(4, 4, 2, mesh.shape["mp"]), ("dp_0", "dp_1", "dp_2", "mp"))
    placed = (
        P(DP, None, "mp"),
        P(DP, None, "mp"),
        P(DP, None, "mp"),
        P(DP, None, "mp"),
        P(DP),
        P(DP),
        P(DP, "mp"),
        P(DP, "mp"),
        P(DP, "mp"),
        P(DP, "mp"),
        P(DP, "mp"),
        P(DP, "mp"),
    )
    return jax.shard_map(
        per_device,
        mesh=split,
        in_specs=placed,
        out_specs=(
            P(DP, "mp"),
            P(DP, "mp"),
            P(DP, "mp"),
            P(DP, "mp"),
            P(DP, "mp"),
            P(DP, "mp"),
            P(),
        ),
        check_vma=False,
    )
```

profile of v0, /device:TPU:2, one launch (start us, length us, event | category | flops | bytes accessed | tf_op | source)
XLA Modules:
  0.0 404.3 jit_solution(1169654670336712328)
XLA Ops:
  7.2 0.0 all-gather.4.cloned.1.call-start
  7.2 0.7 fusion.39
  8.0 1.3 fusion.27
  9.3 0.8 copy.76
  10.2 0.0 all-gather.4.cloned.1.call-update
  10.2 0.0 all-gather.6.cloned.1.call-start
  10.2 0.9 convert_element_type.57
  11.2 0.9 convert_element_type.58
  12.1 0.7 pad_maximum_fusion.1
  12.7 0.0 all-gather.6.cloned.1.call-update
  12.8 0.0 reduce-scatter.5.cloned.1.call-start
  12.8 45.4 %all-gather.4.cloned.1.call-done = bf16[1024,1536]{0,1:T(8,128)(2,1)} async-done(((bf16[1024,192]{0,1:T(8,128)(2,1)}), bf16[1024,1536]{0,1:T(8,128)(2,1)}) %all-gather.4.cloned.1.call-update) | async-done | bytes 3145744 | tf_op jit(solution)/shard_map/all_gather | solution.py:109
  58.3 0.0 copy-start
  58.3 2.7 fusion
  61.0 50.3 %all-gather.6.cloned.1.call-done = bf16[1536,1536]{1,0:T(8,128)(2,1)} async-done(((bf16[48,1536]{1,0:T(8,128)(2,1)}), bf16[1536,1536]{1,0:T(8,128)(2,1)}) %all-gather.6.cloned.1.call-update) | async-done | bytes 4718608 | tf_op jit(solution)/shard_map/all_gather | solution.py:18
  111.3 0.0 copy-done
  111.3 0.0 copy-start.12
  111.3 4.6 %fusion.6 = f32[1024,768]{1,0:T(8,128)S(1)} fusion(bf16[1024,1536]{0,1:T(8,128)(2,1)S(1)} %copy-done, f32[1024]{0:T(1024)S(1)} %add_rsqrt_fusion, bf16[1536,1536]{1,0:T(8,128)(2,1)} %all-gather.6.cloned.1.call-done), kind=kOutput, calls=%fused_computation.14 | convolution fusion | flops 2420637696 | bytes 8654848 | tf_op jit(solution)/shard_map/dot_general | solution.py:121
  115.9 0.0 copy-start.14
  115.9 1.8 copy-done.14
  117.7 0.0 copy-done.12
  117.7 4.4 %multiply_convert_fusion = bf16[1024,1536]{0,1:T(8,128)(2,1)} fusion(bf16[1536,1536]{1,0:T(8,128)(2,1)S(1)} %copy-done.12, f32[1024,768]{1,0:T(8,128)S(1)} %fusion.6), kind=kOutput, calls=%fused_computation.5 | convolution fusion | flops 2426929152 | bytes 8650752 | tf_op jit(solution)/shard_map/dot_general | solution.py:125
  122.1 0.0 copy-start.2
  122.1 0.0 copy-start.3
  122.1 0.0 copy-start.6
  122.1 0.0 copy-start.7
  122.1 0.0 reduce-scatter.5.cloned.1.call-update
  122.1 0.0 all-gather.8.cloned.1.call-start
  122.2 46.7 %reduce-scatter.5.cloned.1.call-done = bf16[1024,192]{0,1:T(8,128)(2,1)} async-done(((bf16[1024,1536]{0,1:T(8,128)(2,1)}), bf16[1024,192]{0,1:T(8,128)(2,1)}) %reduce-scatter.5.cloned.1.call-update) | async-done | bytes 393232 | tf_op jit(solution)/shard_map/reduce_scatter | solution.py:130
  169.0 1.1 reshape.70
  170.1 0.0 copy-done.2
  170.1 0.0 copy-done.3
  170.1 0.0 copy-done.6
  170.1 0.0 copy-done.7
  170.1 1.5 fusion.25
  171.6 0.1 fusion.28
  171.7 0.8 copy.77
  172.5 0.0 all-gather.8.cloned.1.call-update
  172.5 0.2 reduce-scatter.7.cloned.1.call-start
  172.8 44.4 %all-gather.8.cloned.1.call-done = bf16[1024,1536]{0,1:T(8,128)(2,1)} async-done(((bf16[1024,192]{0,1:T(8,128)(2,1)}), bf16[1024,1536]{0,1:T(8,128)(2,1)}) %all-gather.8.cloned.1.call-update) | async-done | bytes 3145744 | tf_op jit(solution)/shard_map/all_gather | solution.py:141
  217.2 8.1 %multiply_convert_fusion.1 = bf16[1024,768]{1,0:T(8,128)(2,1)S(1)} fusion(f32[1024,768]{1,0:T(8,128)} %copy-done.14, bf16[1024,1536]{0,1:T(8,128)(2,1)} %all-gather.8.cloned.1.call-done, bf16[1536,1536]{1,0:T(8,128)(2,1)} %all-gather.6.cloned.1.call-done), kind=kOutput, calls=%fused_computation.11 | convolution fusion | flops 2432434176 | bytes 10223616 | tf_op jit(solution)/shard_map/dot_general | solution.py:142
  225.3 0.0 copy-done.13
  225.3 0.0 copy-start.1
  225.3 5.2 %convolution_multiply_fusion = f32[1536,768]{0,1:T(8,128)S(1)} fusion(bf16[1024,1536]{0,1:T(8,128)(2,1)S(1)} %copy-done.13, f32[1024,768]{1,0:T(8,128)} %copy-done.14), kind=kOutput, calls=%fused_computation.7 | convolution fusion | flops 2424963072 | bytes 11010048 | tf_op jit(solution)/shard_map/dot_general | solution.py:144
  230.5 0.0 copy-done.1
  230.5 2.8 convolution_multiply_fusion.1
  233.3 4.5 %pad_maximum_fusion = f32[1536,1536]{0,1:T(8,128)} fusion(f32[1536,768]{0,1:T(8,128)S(1)} %convolution_multiply_fusion, f32[1536,768]{0,1:T(8,128)S(1)} %convolution_multiply_fusion.1), kind=kLoop, calls=%fused_computation | loop fusion | flops 2359296 | bytes 18874368 | tf_op jit(solution)/shard_map/concatenate | solution.py:30
  237.8 9.6 %copy.73 = f32[1536,1536]{1,0:T(8,128)} copy(f32[1536,1536]{0,1:T(8,128)} %pad_maximum_fusion) | data formatting | bytes 18874368
  247.5 0.0 copy-start.10
  247.5 0.0 copy-start.11
  247.5 0.0 reduce-scatter.7.cloned.1.call-update
  247.5 101.6 %reduce-scatter.7.cloned.1.call-done = f32[48,1536]{1,0:T(8,128)} async-done(((f32[1536,1536]{1,0:T(8,128)}), f32[48,1536]{1,0:T(8,128)}) %reduce-scatter.7.cloned.1.call-update) | async-done | bytes 294928 | tf_op jit(solution)/shard_map/reduce_scatter | solution.py:32
  349.1 1.6 multiply_reduce_fusion
  352.0 9.9 %all-reduce.2 = (f32[]{:T(128)}, f32[]{:T(128)}) all-reduce(f32[]{:T(128)S(6)} %add.97, f32[]{:T(128)} %get-tuple-element.44), channel_id=1, replica_groups=mesh['dp_0'=4,'dp_1'=4,'dp_2'=2,'mp'=8] {'dp_0'}, use_global_device_ids=true, to_apply=%region_5.0 | all-reduce | flops 2 | bytes 16 | tf_op jit(solution)/shard_map/psum | solution.py:37
  361.9 10.1 %all-reduce.1 = (f32[]{:T(128)}, f32[]{:T(128)}) all-reduce(f32[]{:T(128)} %get-tuple-element.34, f32[]{:T(128)} %get-tuple-element.35), channel_id=1, replica_groups=mesh['dp_0'=4,'dp_1'=4,'dp_2'=2,'mp'=8] {'dp_1'}, use_global_device_ids=true, to_apply=%region_6.0 | all-reduce | flops 2 | bytes 16 | tf_op jit(solution)/shard_map/psum | solution.py:37
  372.0 3.1 all-reduce.3
  375.1 18.1 %all-reduce = (f32[]{:T(128)}, f32[]{:T(128)}) all-reduce(f32[]{:T(128)} %get-tuple-element.36, f32[]{:T(128)} %get-tuple-element.37), channel_id=1, replica_groups=mesh['dp_0'=4,'dp_1'=4,'dp_2'=2,'mp'=8] {'mp'}, use_global_device_ids=true, to_apply=%region_8.0 | all-reduce | flops 2 | bytes 16 | tf_op jit(solution)/shard_map/psum | solution.py:37
  394.5 0.0 copy-done.4
  394.5 0.0 copy-done.5
  394.5 0.0 copy-done.8
  394.6 0.0 copy-done.9
  394.6 0.0 copy-done.10
  394.6 0.0 copy-done.11
  394.6 2.0 multiply_subtract_fusion
  (10 shorter events, 0.1 us)
Async XLA Ops:
  7.2 51.1 %all-gather.4.cloned.1.call-start = ((), (), s32[]{:S(2)}) async-start(), calls=%async_computation.2 | async-start | bytes 3538944 | tf_op jit(solution)/shard_map/all_gather | solution.py:109
  10.2 101.2 %all-gather.6.cloned.1.call-start = ((), (), s32[]{:S(2)}) async-start(), calls=%async_computation.3 | async-start | bytes 4866048 | tf_op jit(solution)/shard_map/all_gather | solution.py:18
  12.8 156.2 %reduce-scatter.5.cloned.1.call-start = ((), (), s32[]{:S(2)}) async-start(), calls=%async_computation.4 | async-start | bytes 3538944 | tf_op jit(solution)/shard_map/reduce_scatter | solution.py:130
  58.3 53.1 %copy-start = (bf16[1024,1536]{0,1:T(8,128)(2,1)S(1)}, bf16[1024,1536]{0,1:T(8,128)(2,1)}, u32[]{:S(2)}) copy-start(bf16[1024,1536]{0,1:T(8,128)(2,1)} %all-gather.4.cloned.1.call-done) | copy-start | bytes 9437188
  111.3 6.4 %copy-start.12 = (bf16[1536,1536]{1,0:T(8,128)(2,1)S(1)}, bf16[1536,1536]{1,0:T(8,128)(2,1)}, u32[]{:S(2)}) copy-start(bf16[1536,1536]{1,0:T(8,128)(2,1)} %all-gather.6.cloned.1.call-done) | copy-start | bytes 14155780
  115.9 1.8 copy-start.14
  122.1 48.0 %copy-start.2 = (bf16[4,256,192]{1,2,0:T(8,128)(2,1)S(1)}, bf16[4,256,192]{1,2,0:T(8,128)(2,1)}, u32[]{:S(2)}) copy-start(bf16[4,256,192]{1,2,0:T(8,128)(2,1)} %param.13) | copy-start | bytes 1179652
  122.1 48.0 %copy-start.3 = (bf16[4,256,192]{1,2,0:T(8,128)(2,1)S(1)}, bf16[4,256,192]{1,2,0:T(8,128)(2,1)}, u32[]{:S(2)}) copy-start(bf16[4,256,192]{1,2,0:T(8,128)(2,1)} %param.12) | copy-start | bytes 1179652
  122.1 48.0 %copy-start.6 = (bf16[4,256,192]{1,2,0:T(8,128)(2,1)S(1)}, bf16[4,256,192]{1,2,0:T(8,128)(2,1)}, u32[]{:S(2)}) copy-start(bf16[4,256,192]{1,2,0:T(8,128)(2,1)} %param.14) | copy-start | bytes 1179652
  122.1 48.0 %copy-start.7 = (bf16[4,256,192]{1,2,0:T(8,128)(2,1)S(1)}, bf16[4,256,192]{1,2,0:T(8,128)(2,1)}, u32[]{:S(2)}) copy-start(bf16[4,256,192]{1,2,0:T(8,128)(2,1)} %param.15) | copy-start | bytes 1179652
  122.1 95.1 %all-gather.8.cloned.1.call-start = ((), (), s32[]{:S(2)}) async-start(), calls=%async_computation.5 | async-start | bytes 3538944 | tf_op jit(solution)/shard_map/all_gather | solution.py:141
  172.5 176.6 %reduce-scatter.7.cloned.1.call-start = ((), (), s32[]{:S(2)}) async-start(), calls=%async_computation.6 | async-start | bytes 9732096 | tf_op jit(solution)/shard_map/reduce_scatter | solution.py:32
  217.2 8.1 %copy-start.13 = (bf16[1024,1536]{0,1:T(8,128)(2,1)S(1)}, bf16[1024,1536]{0,1:T(8,128)(2,1)}, u32[]{:S(2)}) copy-start(bf16[1024,1536]{0,1:T(8,128)(2,1)} %all-gather.8.cloned.1.call-done) | copy-start | bytes 9437188
  225.3 5.2 %copy-start.1 = (bf16[1024,1536]{0,1:T(8,128)(2,1)S(1)}, bf16[1024,1536]{0,1:T(8,128)(2,1)}, u32[]{:S(2)}) copy-start(bf16[1024,1536]{0,1:T(8,128)(2,1)} %all-gather.4.cloned.1.call-done) | copy-start | bytes 9437188
  247.5 147.1 %copy-start.4 = (f32[48,768]{1,0:T(8,128)S(1)}, f32[48,768]{1,0:T(8,128)}, u32[]{:S(2)}) copy-start(f32[48,768]{1,0:T(8,128)} %param.19) | copy-start | bytes 442372
  247.5 147.1 %copy-start.5 = (f32[48,768]{1,0:T(8,128)S(1)}, f32[48,768]{1,0:T(8,128)}, u32[]{:S(2)}) copy-start(f32[48,768]{1,0:T(8,128)} %param.18) | copy-start | bytes 442372
  247.5 147.1 %copy-start.8 = (f32[48,768]{1,0:T(8,128)S(1)}, f32[48,768]{1,0:T(8,128)}, u32[]{:S(2)}) copy-start(f32[48,768]{1,0:T(8,128)} %param.21) | copy-start | bytes 442372
  247.5 147.1 %copy-start.9 = (f32[48,768]{1,0:T(8,128)S(1)}, f32[48,768]{1,0:T(8,128)}, u32[]{:S(2)}) copy-start(f32[48,768]{1,0:T(8,128)} %param.23) | copy-start | bytes 442372
  247.5 147.1 %copy-start.10 = (f32[48,768]{1,0:T(8,128)S(1)}, f32[48,768]{1,0:T(8,128)}, u32[]{:S(2)}) copy-start(f32[48,768]{1,0:T(8,128)} %param.22) | copy-start | bytes 442372
  247.5 147.1 %copy-start.11 = (f32[48,768]{1,0:T(8,128)S(1)}, f32[48,768]{1,0:T(8,128)}, u32[]{:S(2)}) copy-start(f32[48,768]{1,0:T(8,128)} %param.20) | copy-start | bytes 442372
Sparse Core Ops, SparseCore 0:
  10.3 47.9 all-gather.3
  61.4 49.9 all-gather.5
  122.2 46.7 reduce-scatter.4
  172.6 44.4 all-gather.7
  247.6 101.4 reduce-scatter.6
where the time goes:
time: 405 us; the launch traced here: 404 us
  waiting for transfers between devices  289 us (71%)
  blocking collectives  41.1 us (10%)
  matrix products  25 us (6%)
  other arithmetic  18.2 us (4%)
  between operations  17.8 us (4%)
  local copies, waits for them, and re-layouts  13.2 us (3%)
    reduce_scatter x1, waiting for transfers between devices, sent_together_2(): lax.psum_scatter(both, axis, scatter_dimension=dim, tiled=True)  102 us
    all_gather x1, waiting for transfers between devices, sent_together(): result, at, outs = (lax.all_gather(both, axis, axis=dim, tiled=True), 0, [])  50.3 us
    reduce_scatter x1, waiting for transfers between devices, per_device(): lax.psum_scatter(partial_value.astype(jnp.bfloat16), 'mp', scatter_dimens...  46.7 us
    all_gather x1, waiting for transfers between devices, per_device(): gathered = lax.all_gather(noisy_rows, 'mp', axis=1, tiled=True)  45.4 us
    all_gather x1, waiting for transfers between devices, per_device(): piece = lax.all_gather(dpred, 'mp', axis=1, tiled=True)  44.4 us
    psum x4, blocking collectives, by_axis(): return functools.reduce(lax.psum, axes, shard)  41.1 us
    unnamed x31, local copies, waits for them, and re-layouts  11.5 us
  transfers between devices with their start and end apart: 5, of which 5 were waited for; matrix products, arithmetic and copies ran while one was open for 1% of the time, Pallas kernels for 0%

commit v1 on v0

--- a/solution.py
+++ b/solution.py
@@ -11,6 +11,16 @@
 adam_count = 100.0
 learn_rate = 0.05
 decay_rate = 0.01
+
+
+def gather_around(x, axis, dim):
+    ways, here, step = (lax.axis_size(axis), lax.axis_index(axis), x.shape[dim])
+    dims = [n * ways if d == dim else n for d, n in enumerate(x.shape)]
+    full = lax.dynamic_update_slice_in_dim(jnp.zeros(dims, x.dtype), x, here * step, axis=dim)
+    for far in range(1, ways):
+        x = lax.ppermute(x, axis, [(d, (d + 1) % ways) for d in range(ways)])
+        full = lax.dynamic_update_slice_in_dim(full, x, (here - far) % ways * step, axis=dim)
+    return full
 
 
 def sent_together(arrays, axis, dim, along):
@@ -138,7 +148,7 @@
         .astype(jnp.bfloat16)
         .reshape(row_count, width_local)
     )
-    piece = lax.all_gather(dpred, "mp", axis=1, tiled=True)
+    piece = gather_around(dpred, "mp", 1)
     summed = jnp.dot(piece, down_full, preferred_element_type=jnp.float32)
     grad_piece = (
         lax.dot_general(piece, hidden, (((0,), (0,)), ((), ())), preferred_element_type=jnp.float32)

time: 405 us -> 433 us (1.069)
  waiting for transfers between devices: 289 us -> 320 us
  matrix products: 25 us -> 19.4 us
    ppermute x0 -> x7, waiting for transfers between devices: none -> 74.2 us  [gather_around(): x = lax.ppermute(x, axis, [(d, (d + 1) % ways) for d in range(ways)])]
    all_gather x1 -> x0, waiting for transfers between devices: 44.4 us -> none  [per_device(): piece = lax.all_gather(dpred, 'mp', axis=1, tiled=True)]
    unnamed x31 -> x41, local copies, waits for them, and re-layouts: 11.5 us -> 12 us
  transfers between devices with their start and end apart: 5 -> 11, of which waited for: 5 -> 11; matrix products, arithmetic and copies ran while one was open for 1% -> 1% of each run, Pallas kernels for 0% -> 0%
where the time goes in v1:
time: 433 us
  waiting for transfers between devices  320 us (74%)
  blocking collectives  41.1 us (9%)
  matrix products  19.4 us (4%)
  other arithmetic  18.7 us (4%)
  between operations  18 us (4%)
  local copies, waits for them, and re-layouts  13.7 us (3%)
    reduce_scatter x1, waiting for transfers between devices, sent_together_2(): lax.psum_scatter(both, axis, scatter_dimension=dim, tiled=True)  103 us
    ppermute x7, waiting for transfers between devices, gather_around(): x = lax.ppermute(x, axis, [(d, (d + 1) % ways) for d in range(ways)])  74.2 us
    all_gather x1, waiting for transfers between devices, sent_together(): result, at, outs = (lax.all_gather(both, axis, axis=dim, tiled=True), 0, [])  50.3 us
    reduce_scatter x1, waiting for transfers between devices, per_device(): lax.psum_scatter(partial_value.astype(jnp.bfloat16), 'mp', scatter_dimens...  46.3 us
    all_gather x1, waiting for transfers between devices, per_device(): gathered = lax.all_gather(noisy_rows, 'mp', axis=1, tiled=True)  45.4 us
    psum x4, blocking collectives, by_axis(): return functools.reduce(lax.psum, axes, shard)  41.1 us
    unnamed x41, local copies, waits for them, and re-layouts  12 us
  transfers between devices with their start and end apart: 11, of which 11 were waited for; matrix products, arithmetic and copies ran while one was open for 1% of the time, Pallas kernels for 0%

profile of v1, /device:TPU:2, one launch (start us, length us, event | category | flops | bytes accessed | tf_op | source)
XLA Modules:
  0.0 433.0 jit_solution(5566452543630471601)
XLA Ops:
  7.2 0.0 all-gather.3.cloned.1.call-start
  7.2 1.2 fusion.39
  8.5 1.3 fusion.27
  9.8 0.8 copy.76
  10.7 0.0 all-gather.3.cloned.1.call-update
  10.7 0.0 all-gather.5.cloned.1.call-start
  10.8 0.9 convert_element_type.57
  11.7 0.9 convert_element_type.58
  12.6 0.7 pad_maximum_fusion.1
  13.3 0.0 all-gather.5.cloned.1.call-update
  13.3 0.0 reduce-scatter.5.cloned.1.call-start
  13.4 45.4 %all-gather.3.cloned.1.call-done = bf16[1024,1536]{0,1:T(8,128)(2,1)} async-done(((bf16[1024,192]{0,1:T(8,128)(2,1)}), bf16[1024,1536]{0,1:T(8,128)(2,1)}) %all-gather.3.cloned.1.call-update) | async-done | bytes 3145744 | tf_op jit(solution)/shard_map/all_gather | solution.py:119
  58.8 2.7 fusion
  61.6 50.3 %all-gather.5.cloned.1.call-done = bf16[1536,1536]{1,0:T(8,128)(2,1)} async-done(((bf16[48,1536]{1,0:T(8,128)(2,1)}), bf16[1536,1536]{1,0:T(8,128)(2,1)}) %all-gather.5.cloned.1.call-update) | async-done | bytes 4718608 | tf_op jit(solution)/shard_map/all_gather | solution.py:28
  111.9 4.6 %fusion.6 = f32[1024,768]{1,0:T(8,128)S(1)} fusion(bf16[1024,1536]{0,1:T(8,128)(2,1)S(1)} %copy-done, f32[1024]{0:T(1024)S(1)} %add_rsqrt_fusion, bf16[1536,1536]{1,0:T(8,128)(2,1)} %all-gather.5.cloned.1.call-done), kind=kOutput, calls=%fused_computation.14 | convolution fusion | flops 2420637696 | bytes 8654848 | tf_op jit(solution)/shard_map/dot_general | solution.py:131
  116.5 1.7 copy-done.16
  118.2 4.4 %multiply_convert_fusion = bf16[1024,1536]{0,1:T(8,128)(2,1)} fusion(bf16[1536,1536]{1,0:T(8,128)(2,1)S(1)} %copy-done.15, f32[1024,768]{1,0:T(8,128)S(1)} %fusion.6), kind=kOutput, calls=%fused_computation.5 | convolution fusion | flops 2426929152 | bytes 8650752 | tf_op jit(solution)/shard_map/dot_general | solution.py:135
  122.6 0.0 copy-start.6
  122.6 0.0 copy-start.7
  122.6 0.0 copy-start.12
  122.6 0.0 reduce-scatter.5.cloned.1.call-update
  122.7 0.0 reduce-scatter.7.cloned.1.call-start
  122.7 0.5 copy-done.14
  123.3 46.3 %reduce-scatter.5.cloned.1.call-done = bf16[1024,192]{0,1:T(8,128)(2,1)} async-done(((bf16[1024,1536]{0,1:T(8,128)(2,1)}), bf16[1024,192]{0,1:T(8,128)(2,1)}) %reduce-scatter.5.cloned.1.call-update) | async-done | bytes 393232 | tf_op jit(solution)/shard_map/reduce_scatter | solution.py:140
  169.6 1.1 reshape.70
  170.7 0.0 copy-done.2
  170.7 0.0 copy-done.3
  170.7 0.0 copy-done.6
  170.7 0.0 copy-done.7
  170.7 0.0 copy-done.12
  170.7 1.5 fusion.25
  172.2 0.1 fusion.28
  172.4 0.8 collective-permute-start
  173.2 8.6 %collective-permute-done = bf16[1024,192]{0,1:T(8,128)(2,1)S(1)} collective-permute-done((bf16[1024,192]{0,1:T(8,128)(2,1)S(1)}, bf16[1024,192]{0,1:T(8,128)(2,1)S(1)}, u32[]{:S(2)}, u32[]{:S(2)}) %collective-permute-start) | collective-permute-done | bytes 393248 | tf_op jit(solution)/shard_map/ppermute | solution.py:21
  181.8 0.1 collective-permute-start.1
  181.9 10.3 %collective-permute-done.1 = bf16[1024,192]{0,1:T(8,128)(2,1)S(1)} collective-permute-done((bf16[1024,192]{0,1:T(8,128)(2,1)S(1)}, bf16[1024,192]{0,1:T(8,128)(2,1)S(1)}, u32[]{:S(2)}, u32[]{:S(2)}) %collective-permute-start.1) | collective-permute-done | bytes 393248 | tf_op jit(solution)/shard_map/ppermute | solution.py:21
  192.2 0.5 collective-permute-start.2
  192.6 11.1 %collective-permute-done.2 = bf16[1024,192]{0,1:T(8,128)(2,1)S(1)} collective-permute-done((bf16[1024,192]{0,1:T(8,128)(2,1)S(1)}, bf16[1024,192]{0,1:T(8,128)(2,1)S(1)}, u32[]{:S(2)}, u32[]{:S(2)}) %collective-permute-start.2) | collective-permute-done | bytes 393248 | tf_op jit(solution)/shard_map/ppermute | solution.py:21
  203.7 0.8 collective-permute-start.3
  204.5 11.9 %collective-permute-done.3 = bf16[1024,192]{0,1:T(8,128)(2,1)S(1)} collective-permute-done((bf16[1024,192]{0,1:T(8,128)(2,1)S(1)}, bf16[1024,192]{0,1:T(8,128)(2,1)S(1)}, u32[]{:S(2)}, u32[]{:S(2)}) %collective-permute-start.3) | collective-permute-done | bytes 393248 | tf_op jit(solution)/shard_map/ppermute | solution.py:21
  216.4 0.1 collective-permute-start.4
  216.5 12.5 %collective-permute-done.4 = bf16[1024,192]{0,1:T(8,128)(2,1)S(1)} collective-permute-done((bf16[1024,192]{0,1:T(8,128)(2,1)S(1)}, bf16[1024,192]{0,1:T(8,128)(2,1)S(1)}, u32[]{:S(2)}, u32[]{:S(2)}) %collective-permute-start.4) | collective-permute-done | bytes 393248 | tf_op jit(solution)/shard_map/ppermute | solution.py:21
  228.9 0.0 collective-permute-start.5
  228.9 0.4 broadcast_in_dim.2
  229.5 11.2 %collective-permute-done.5 = bf16[1024,192]{0,1:T(8,128)(2,1)S(1)} collective-permute-done((bf16[1024,192]{0,1:T(8,128)(2,1)S(1)}, bf16[1024,192]{0,1:T(8,128)(2,1)S(1)}, u32[]{:S(2)}, u32[]{:S(2)}) %collective-permute-start.5) | collective-permute-done | bytes 393248 | tf_op jit(solution)/shard_map/ppermute | solution.py:21
  240.7 0.0 collective-permute-start.6
  240.8 0.0 slice-start
  240.8 8.8 %collective-permute-done.6 = bf16[1024,192]{0,1:T(8,128)(2,1)S(1)} collective-permute-done((bf16[1024,192]{0,1:T(8,128)(2,1)S(1)}, bf16[1024,192]{0,1:T(8,128)(2,1)S(1)}, u32[]{:S(2)}, u32[]{:S(2)}) %collective-permute-start.6) | collective-permute-done | bytes 393248 | tf_op jit(solution)/shard_map/ppermute | solution.py:21
  249.7 0.0 slice-start.1
  249.7 3.2 convolution_multiply_fusion
  252.9 4.5 %multiply_convert_fusion.1 = bf16[1024,768]{1,0:T(8,128)(2,1)S(1)} fusion(f32[1024,768]{1,0:T(8,128)S(1)} %copy-done.17, bf16[1024,1536]{0,1:T(8,128)(2,1)S(1)} %constant_dynamic-update-slice_fusion, bf16[1536,1536]{1,0:T(8,128)(2,1)S(1)} %bitcast.21), kind=kOutput, calls=%fused_computation.11 | convolution fusion | flops 2432434176 | bytes 10223616 | tf_op jit(solution)/shard_map/dot_general | solution.py:152
  257.5 2.8 convolution_multiply_fusion.1
  260.2 4.5 %pad_maximum_fusion = f32[1536,1536]{0,1:T(8,128)} fusion(f32[1536,768]{0,1:T(8,128)S(1)} %convolution_multiply_fusion, f32[1536,768]{0,1:T(8,128)S(1)} %convolution_multiply_fusion.1), kind=kLoop, calls=%fused_computation | loop fusion | flops 2359296 | bytes 18874368 | tf_op jit(solution)/shard_map/concatenate | solution.py:40
  264.8 9.7 %copy.73 = f32[1536,1536]{1,0:T(8,128)} copy(f32[1536,1536]{0,1:T(8,128)} %pad_maximum_fusion) | data formatting | bytes 18874368
  274.4 0.0 copy-start.10
  274.4 0.0 copy-start.11
  274.4 0.0 reduce-scatter.7.cloned.1.call-update
  274.5 103.4 %reduce-scatter.7.cloned.1.call-done = f32[48,1536]{1,0:T(8,128)} async-done(((f32[1536,1536]{1,0:T(8,128)}), f32[48,1536]{1,0:T(8,128)}) %reduce-scatter.7.cloned.1.call-update) | async-done | bytes 294928 | tf_op jit(solution)/shard_map/reduce_scatter | solution.py:42
  377.8 1.6 multiply_reduce_fusion
  380.8 9.9 %all-reduce.2 = (f32[]{:T(128)}, f32[]{:T(128)}) all-reduce(f32[]{:T(128)S(6)} %add.165, f32[]{:T(128)} %get-tuple-element.44), channel_id=1, replica_groups=mesh['dp_0'=4,'dp_1'=4,'dp_2'=2,'mp'=8] {'dp_0'}, use_global_device_ids=true, to_apply=%region_5.6 | all-reduce | flops 2 | bytes 16 | tf_op jit(solution)/shard_map/psum | solution.py:47
  390.6 10.1 %all-reduce.1 = (f32[]{:T(128)}, f32[]{:T(128)}) all-reduce(f32[]{:T(128)} %get-tuple-element.34, f32[]{:T(128)} %get-tuple-element.35), channel_id=1, replica_groups=mesh['dp_0'=4,'dp_1'=4,'dp_2'=2,'mp'=8] {'dp_1'}, use_global_device_ids=true, to_apply=%region_6.7 | all-reduce | flops 2 | bytes 16 | tf_op jit(solution)/shard_map/psum | solution.py:47
  400.7 3.1 all-reduce.3
  403.8 18.1 %all-reduce = (f32[]{:T(128)}, f32[]{:T(128)}) all-reduce(f32[]{:T(128)} %get-tuple-element.36, f32[]{:T(128)} %get-tuple-element.37), channel_id=1, replica_groups=mesh['dp_0'=4,'dp_1'=4,'dp_2'=2,'mp'=8] {'mp'}, use_global_device_ids=true, to_apply=%region_8.9 | all-reduce | flops 2 | bytes 16 | tf_op jit(solution)/shard_map/psum | solution.py:47
  423.3 2.0 multiply_subtract_fusion
  (41 shorter events, 0.5 us)
Async XLA Ops:
  7.2 51.6 %all-gather.3.cloned.1.call-start = ((), (), s32[]{:S(2)}) async-start(), calls=%async_computation.2 | async-start | bytes 3538944 | tf_op jit(solution)/shard_map/all_gather | solution.py:119
  10.7 101.2 %all-gather.5.cloned.1.call-start = ((), (), s32[]{:S(2)}) async-start(), calls=%async_computation.3 | async-start | bytes 4866048 | tf_op jit(solution)/shard_map/all_gather | solution.py:28
  13.3 156.3 %reduce-scatter.5.cloned.1.call-start = ((), (), s32[]{:S(2)}) async-start(), calls=%async_computation.4 | async-start | bytes 3538944 | tf_op jit(solution)/shard_map/reduce_scatter | solution.py:140
  58.8 53.1 %copy-start = (bf16[1024,1536]{0,1:T(8,128)(2,1)S(1)}, bf16[1024,1536]{0,1:T(8,128)(2,1)}, u32[]{:S(2)}) copy-start(bf16[1024,1536]{0,1:T(8,128)(2,1)} %all-gather.3.cloned.1.call-done) | copy-start | bytes 9437188
  111.9 6.3 %copy-start.15 = (bf16[1536,1536]{1,0:T(8,128)(2,1)S(1)}, bf16[1536,1536]{1,0:T(8,128)(2,1)}, u32[]{:S(2)}) copy-start(bf16[1536,1536]{1,0:T(8,128)(2,1)} %all-gather.5.cloned.1.call-done) | copy-start | bytes 14155780
  116.5 1.8 copy-start.16
  122.6 0.7 copy-start.14
  122.6 0.7 copy-start.13
  122.6 48.1 %copy-start.2 = (bf16[4,256,192]{1,2,0:T(8,128)(2,1)S(1)}, bf16[4,256,192]{1,2,0:T(8,128)(2,1)}, u32[]{:S(2)}) copy-start(bf16[4,256,192]{1,2,0:T(8,128)(2,1)} %param.13) | copy-start | bytes 1179652
  122.6 48.1 %copy-start.3 = (bf16[4,256,192]{1,2,0:T(8,128)(2,1)S(1)}, bf16[4,256,192]{1,2,0:T(8,128)(2,1)}, u32[]{:S(2)}) copy-start(bf16[4,256,192]{1,2,0:T(8,128)(2,1)} %param.12) | copy-start | bytes 1179652
  122.6 48.1 %copy-start.6 = (bf16[4,256,192]{1,2,0:T(8,128)(2,1)S(1)}, bf16[4,256,192]{1,2,0:T(8,128)(2,1)}, u32[]{:S(2)}) copy-start(bf16[4,256,192]{1,2,0:T(8,128)(2,1)} %param.14) | copy-start | bytes 1179652
  122.6 48.1 %copy-start.7 = (bf16[4,256,192]{1,2,0:T(8,128)(2,1)S(1)}, bf16[4,256,192]{1,2,0:T(8,128)(2,1)}, u32[]{:S(2)}) copy-start(bf16[4,256,192]{1,2,0:T(8,128)(2,1)} %param.15) | copy-start | bytes 1179652
  122.6 48.1 %copy-start.12 = (f32[4]{0:T(128)S(1)}, f32[4]{0:T(128)}, u32[]{:S(2)}) copy-start(f32[4]{0:T(128)} %get-tuple-element.48) | copy-start | bytes 52
  122.7 255.2 %reduce-scatter.7.cloned.1.call-start = ((), (), s32[]{:S(2)}) async-start(), calls=%async_computation.5 | async-start | bytes 9732096 | tf_op jit(solution)/shard_map/reduce_scatter | solution.py:42
  172.4 9.4 %collective-permute-start = (bf16[1024,192]{0,1:T(8,128)(2,1)S(1)}, bf16[1024,192]{0,1:T(8,128)(2,1)S(1)}, u32[]{:S(2)}, u32[]{:S(2)}) collective-permute-start(bf16[1024,192]{0,1:T(8,128)(2,1)S(1)} %bitcast.18), channel_id=1, source_target_pairs={{0,1},{1,2},{2,3},{3,4},{4,5},{5,6},{6,7},{7,0},{8,9},{9,10},{10,1... | collective-permute-start | bytes 1179656 | tf_op jit(solution)/shard_map/ppermute | solution.py:21
  181.8 10.4 %collective-permute-start.1 = (bf16[1024,192]{0,1:T(8,128)(2,1)S(1)}, bf16[1024,192]{0,1:T(8,128)(2,1)S(1)}, u32[]{:S(2)}, u32[]{:S(2)}) collective-permute-start(bf16[1024,192]{0,1:T(8,128)(2,1)S(1)} %collective-permute-done), channel_id=1, source_target_pairs={{0,1},{1,2},{2,3},{3,4},{4,5},{5,6},{6,7},{7,0},{8,9},{9,10},{10,1... | collective-permute-start | bytes 1179656 | tf_op jit(solution)/shard_map/ppermute | solution.py:21
  192.2 11.5 %collective-permute-start.2 = (bf16[1024,192]{0,1:T(8,128)(2,1)S(1)}, bf16[1024,192]{0,1:T(8,128)(2,1)S(1)}, u32[]{:S(2)}, u32[]{:S(2)}) collective-permute-start(bf16[1024,192]{0,1:T(8,128)(2,1)S(1)} %collective-permute-done.1), channel_id=1, source_target_pairs={{0,1},{1,2},{2,3},{3,4},{4,5},{5,6},{6,7},{7,0},{8,9},{9,10},{10,1... | collective-permute-start | bytes 1179656 | tf_op jit(solution)/shard_map/ppermute | solution.py:21
  203.7 12.7 %collective-permute-start.3 = (bf16[1024,192]{0,1:T(8,128)(2,1)S(1)}, bf16[1024,192]{0,1:T(8,128)(2,1)S(1)}, u32[]{:S(2)}, u32[]{:S(2)}) collective-permute-start(bf16[1024,192]{0,1:T(8,128)(2,1)S(1)} %collective-permute-done.2), channel_id=1, source_target_pairs={{0,1},{1,2},{2,3},{3,4},{4,5},{5,6},{6,7},{7,0},{8,9},{9,10},{10,1... | collective-permute-start | bytes 1179656 | tf_op jit(solution)/shard_map/ppermute | solution.py:21
  216.4 12.6 %collective-permute-start.4 = (bf16[1024,192]{0,1:T(8,128)(2,1)S(1)}, bf16[1024,192]{0,1:T(8,128)(2,1)S(1)}, u32[]{:S(2)}, u32[]{:S(2)}) collective-permute-start(bf16[1024,192]{0,1:T(8,128)(2,1)S(1)} %collective-permute-done.3), channel_id=1, source_target_pairs={{0,1},{1,2},{2,3},{3,4},{4,5},{5,6},{6,7},{7,0},{8,9},{9,10},{10,1... | collective-permute-start | bytes 1179656 | tf_op jit(solution)/shard_map/ppermute | solution.py:21
  228.9 11.7 %collective-permute-start.5 = (bf16[1024,192]{0,1:T(8,128)(2,1)S(1)}, bf16[1024,192]{0,1:T(8,128)(2,1)S(1)}, u32[]{:S(2)}, u32[]{:S(2)}) collective-permute-start(bf16[1024,192]{0,1:T(8,128)(2,1)S(1)} %collective-permute-done.4), channel_id=1, source_target_pairs={{0,1},{1,2},{2,3},{3,4},{4,5},{5,6},{6,7},{7,0},{8,9},{9,10},{10,1... | collective-permute-start | bytes 1179656 | tf_op jit(solution)/shard_map/ppermute | solution.py:21
  229.3 20.3 %copy-start.17 = (f32[1024,768]{1,0:T(8,128)S(1)}, f32[1024,768]{1,0:T(8,128)}, u32[]{:S(2)}) copy-start(f32[1024,768]{1,0:T(8,128)} %copy-done.16) | copy-start | bytes 9437188
  240.7 9.0 %collective-permute-start.6 = (bf16[1024,192]{0,1:T(8,128)(2,1)S(1)}, bf16[1024,192]{0,1:T(8,128)(2,1)S(1)}, u32[]{:S(2)}, u32[]{:S(2)}) collective-permute-start(bf16[1024,192]{0,1:T(8,128)(2,1)S(1)} %collective-permute-done.5), channel_id=1, source_target_pairs={{0,1},{1,2},{2,3},{3,4},{4,5},{5,6},{6,7},{7,0},{8,9},{9,10},{10,1... | collective-permute-start | bytes 1179656 | tf_op jit(solution)/shard_map/ppermute | solution.py:21
  240.8 12.1 %slice-start = ((s8[4718592]{0:T(1024)(128)(4,1)}), s8[524288]{0:T(1024)(128)(4,1)S(1)}, s32[]{:S(2)}) async-start(s8[4718592]{0:T(1024)(128)(4,1)} %bitcast.20), calls=%async_computation.6 | async-start | bytes 1048576
  249.7 3.2 slice-start.1
  252.9 4.5 %copy-start.1 = (bf16[1024,1536]{0,1:T(8,128)(2,1)S(1)}, bf16[1024,1536]{0,1:T(8,128)(2,1)}, u32[]{:S(2)}) copy-start(bf16[1024,1536]{0,1:T(8,128)(2,1)} %all-gather.3.cloned.1.call-done) | copy-start | bytes 9437188
  274.4 148.8 %copy-start.4 = (f32[48,768]{1,0:T(8,128)S(1)}, f32[48,768]{1,0:T(8,128)}, u32[]{:S(2)}) copy-start(f32[48,768]{1,0:T(8,128)} %param.19) | copy-start | bytes 442372
  274.4 148.8 %copy-start.5 = (f32[48,768]{1,0:T(8,128)S(1)}, f32[48,768]{1,0:T(8,128)}, u32[]{:S(2)}) copy-start(f32[48,768]{1,0:T(8,128)} %param.18) | copy-start | bytes 442372
  274.4 148.8 %copy-start.8 = (f32[48,768]{1,0:T(8,128)S(1)}, f32[48,768]{1,0:T(8,128)}, u32[]{:S(2)}) copy-start(f32[48,768]{1,0:T(8,128)} %param.21) | copy-start | bytes 442372
  274.4 148.8 %copy-start.9 = (f32[48,768]{1,0:T(8,128)S(1)}, f32[48,768]{1,0:T(8,128)}, u32[]{:S(2)}) copy-start(f32[48,768]{1,0:T(8,128)} %param.23) | copy-start | bytes 442372
  274.4 148.8 %copy-start.10 = (f32[48,768]{1,0:T(8,128)S(1)}, f32[48,768]{1,0:T(8,128)}, u32[]{:S(2)}) copy-start(f32[48,768]{1,0:T(8,128)} %param.22) | copy-start | bytes 442372
  274.4 148.8 %copy-start.11 = (f32[48,768]{1,0:T(8,128)S(1)}, f32[48,768]{1,0:T(8,128)}, u32[]{:S(2)}) copy-start(f32[48,768]{1,0:T(8,128)} %param.20) | copy-start | bytes 442372
Sparse Core Ops, SparseCore 0:
  10.8 47.9 all-gather.2
  61.9 49.9 all-gather.4
  122.8 46.7 reduce-scatter.4
  274.6 103.1 reduce-scatter.6
